TPU v7x, 512 devices: a 8x2x16 block of a 8x8x16 slice. The times are simulated.
512 devices in a mesh: runs: 2 (over y), gx: 16 (over z), gy: 8 (over x), gz: 2 (over core).
Axes of the slice: x: 8, y: 2, z: 16, core: 2. Of those that a mesh axis runs over, the one named last changes fastest.
The devices are a block of a 8x8x16 slice.
Arguments:
- positions: float32 [3, 8, 65536], P(None, None, ('runs', 'gx', 'gy', 'gz')), parts along dimension 2, as said below
- velocities: float32 [3, 8, 65536], P(None, None, ('runs', 'gx', 'gy', 'gz')), parts along dimension 2, may hold values from -5 to 5
- send_list: int32 [91136], P(('runs', 'gx', 'gy', 'gz')), parts along dimension 0, may hold values from 0 to 127
- pair_list: int32 [2, 917504], P(None, ('runs', 'gx', 'gy', 'gz')), parts along dimension 1, may hold values from 0 to 306, as said below
- constraint_flags: int32 [7, 65536], P(None, ('runs', 'gx', 'gy', 'gz')), parts along dimension 1, may hold values 0 or 1
Outputs:
- final_positions: float32 [3, 8, 65536], P(None, None, ('runs', 'gx', 'gy', 'gz')), parts along dimension 2
- final_velocities: float32 [3, 8, 65536], P(None, None, ('runs', 'gx', 'gy', 'gz')), parts along dimension 2
- energies: float32 [6, 2], P('runs'), parts along dimension 0
There are 2 independent parts, one for each index of `runs`. A program takes and returns all parts, laid end to end along the dimension named above; each array names one. Nothing has to cross between parts.
Inputs may be any that keep to these rules, and one draw needn't show every extreme that they name: `pair_list`: each domain's 1792 slots name clusters of its extended set: 0 to 127 its own, then its received zone blocks in order; padding slots hold 306 in both rows; every cluster appears in a slot with itself; no unordered pair appears twice. `positions`: eight beads of a cluster lie in its cell of side 1, the cells of a domain filling a box of 1 by 8 by 16; neighbouring beads of a cluster are between 0.25 and 0.6 apart.
All inputs are finite; a program needn't handle non-finite values. No bound on the sum of `constraint_flags` on one device may be relied on, other than what follows from the above.
Results may differ from a plain program's by a relative error of at most 0.0003.
Values sent between devices are 32-bit elements; how exact they have to be, the bound alone decides.
A program may use at most 64 MiB of HBM per device.

v0:
```python
import jax
import jax.numpy as jnp
import numpy as np
from jax import lax
from jax.sharding import PartitionSpec as P

CX = 1
CY = 8
CZ = 16
ITERS = 3
NORDER = 4
time_step = 0.02
strength = 2.0
root_half = 0.7071067811865476
zone_list = ((1, 0, 0), (0, 1, 0), (0, 0, 1), (1, 1, 0), (1, 0, 1), (0, 1, 1), (1, 1, 1))


def from_behind(value, axis, by):
    count = lax.axis_size(axis)
    return lax.ppermute(value, axis, [(i, (i + by) % count) for i in range(count)])


def over_axes(value, axes):
    for axis in axes:
        value = lax.psum(value, axis)
    return value


def zone_sizes():
    return tuple(
        (
            (CX if direction[0] == 0 else 1)
            * (CY if direction[1] == 0 else 1)
            * (CZ if direction[2] == 0 else 1)
            for direction in zone_list
        )
    )


def split_blocks(packed, block_sizes):
    pieces = []
    position = 0
    for length in block_sizes:
        pieces.append(packed[:, :, position : position + length])
        position += length
    return pieces


def shell_offsets():
    block_sizes = zone_sizes()
    columns = []
    for number in range(7):
        direction = zone_list[number]
        column = np.array(
            [[direction[0] * CX], [direction[1] * CY], [direction[2] * CZ]], np.float32
        )
        columns.append(np.tile(column, (1, block_sizes[number])))
    return jnp.asarray(np.concatenate(columns, axis=1))[:, None, :]


def share_coords(coords, send_list):
    sizes_all = zone_sizes()
    outgoing = split_blocks(jnp.take(coords, send_list, axis=2), sizes_all)
    along_y = from_behind(
        jnp.concatenate([outgoing[1], outgoing[3], outgoing[5], outgoing[6]], axis=2), "gy", -1
    )
    got_y = split_blocks(along_y, [sizes_all[1], sizes_all[3], sizes_all[5], sizes_all[6]])
    along_x = from_behind(
        jnp.concatenate([outgoing[0], outgoing[4], got_y[1], got_y[3]], axis=2), "gx", -1
    )
    got_x = split_blocks(along_x, [sizes_all[0], sizes_all[4], sizes_all[3], sizes_all[6]])
    along_z = from_behind(
        jnp.concatenate([outgoing[2], got_x[1], got_y[2], got_x[3]], axis=2), "gz", -1
    )
    got_z = split_blocks(along_z, [sizes_all[2], sizes_all[4], sizes_all[5], sizes_all[6]])
    received = [got_x[0], got_y[0], got_z[0], got_x[2], got_z[1], got_z[2], got_z[3]]
    return jnp.concatenate(received, axis=2) + shell_offsets()


def return_forces(halo_forces):
    sizes_all = zone_sizes()
    outgoing = split_blocks(halo_forces, sizes_all)
    along_z = from_behind(
        jnp.concatenate([outgoing[2], outgoing[4], outgoing[5], outgoing[6]], axis=2), "gz", 1
    )
    got_z = split_blocks(along_z, [sizes_all[2], sizes_all[4], sizes_all[5], sizes_all[6]])
    along_x = from_behind(
        jnp.concatenate([outgoing[0], outgoing[3], got_z[1], got_z[3]], axis=2), "gx", 1
    )
    got_x = split_blocks(along_x, [sizes_all[0], sizes_all[3], sizes_all[4], sizes_all[6]])
    settled = [got_x[0], got_z[0], got_x[2]]
    pending = [got_x[1], got_z[2], got_x[3]]
    along_y = from_behind(
        jnp.concatenate([outgoing[1], pending[0], pending[1], pending[2]], axis=2), "gy", 1
    )
    got_y = split_blocks(along_y, [sizes_all[1], sizes_all[3], sizes_all[5], sizes_all[6]])
    return jnp.concatenate(
        [settled[0], got_y[0], settled[1], got_y[1], settled[2], got_y[2], got_y[3]], axis=2
    )


def pair_tables(pair_list, extended_count):
    rows = lax.broadcasted_iota(jnp.int32, (extended_count, pair_list.shape[1]), 0)
    first_table = (rows == pair_list[0][None, :]).astype(jnp.float32)
    second_table = (rows == pair_list[1][None, :]).astype(jnp.float32)
    return (first_table, second_table)


def domain_forces(extended, pair_list, tables):
    extended_count = extended.shape[2]
    slot_count = pair_list.shape[1]
    first_ids = pair_list[0]
    second_ids = pair_list[1]
    flat = extended.reshape(24, extended_count)
    first_coords = jnp.dot(flat, tables[0], precision=lax.Precision.HIGHEST).reshape(
        3, 8, slot_count
    )
    second_coords = jnp.dot(flat, tables[1], precision=lax.Precision.HIGHEST).reshape(
        3, 8, slot_count
    )
    separation = first_coords[:, :, None, :] - second_coords[:, None, :, :]
    scaled = jnp.sum(separation * separation, axis=0)
    intersect = jnp.maximum(1.0 - scaled, 0.0)
    bead_row = lax.broadcasted_iota(jnp.int32, (8, 8, 1), 0)
    bead_column = lax.broadcasted_iota(jnp.int32, (8, 8, 1), 1)
    self_pair = (first_ids == second_ids)[None, None, :]
    usable = (first_ids < extended_count - 1)[None, None, :]
    weight = (jnp.where(self_pair, bead_row < bead_column, True) & usable).astype(jnp.float32)
    energy = strength * jnp.sum(weight * intersect * intersect * intersect)
    magnitude = 6.0 * strength * weight * intersect * intersect
    pushing = magnitude[None] * separation
    on_first = jnp.sum(pushing, axis=2).reshape(24, slot_count)
    on_second = (-jnp.sum(pushing, axis=1)).reshape(24, slot_count)
    contract = (((1,), (1,)), ((), ()))
    forces = lax.dot_general(on_first, tables[0], contract, precision=lax.Precision.HIGHEST)
    forces = forces + lax.dot_general(
        on_second, tables[1], contract, precision=lax.Precision.HIGHEST
    )
    return (forces.reshape(3, 8, extended_count), energy)


def local_forces(coords, send_list, pair_list, tables):
    halo_coords = share_coords(coords, send_list)
    dummy_cluster = jnp.zeros((3, 8, 1), jnp.float32)
    extended = jnp.concatenate([coords, halo_coords, dummy_cluster], axis=2)
    forces, energy = domain_forces(extended, pair_list, tables)
    cluster_count = coords.shape[2]
    returned = return_forces(forces[:, :, cluster_count : cluster_count + send_list.shape[0]])
    home_forces = forces[:, :, :cluster_count].at[:, :, send_list].add(returned)
    return (home_forces, energy)


def link_vectors(coords):
    return coords[:, :-1, :] - coords[:, 1:, :]


def link_lengths(coords):
    vectors = link_vectors(coords)
    return jnp.sqrt(jnp.sum(vectors * vectors, axis=0))


def expand(coupling, source):
    coupling_down = jnp.pad(coupling, ((1, 0), (0, 0)))
    coupling_up = jnp.pad(coupling, ((0, 1), (0, 0)))
    series = source
    result = source
    for expansion in range(NORDER):
        series = (
            coupling_down * jnp.pad(series, ((1, 0), (0, 0)))[:-1]
            + coupling_up * jnp.pad(series, ((0, 1), (0, 0)))[1:]
        )
        result = result + series
    return result


def apply_links(coords, directions, solution):
    shifts = directions * (root_half * solution)[None]
    return (
        coords
        - jnp.pad(shifts, ((0, 0), (0, 1), (0, 0)))
        + jnp.pad(shifts, ((0, 0), (1, 0), (0, 0)))
    )


def constrain(previous, updated, rest_length, link_flags):
    old_vectors = link_vectors(previous)
    directions = (
        old_vectors / jnp.maximum(jnp.sqrt(jnp.sum(old_vectors * old_vectors, axis=0)), 0.2)[None]
    )
    coupling = (
        0.5
        * jnp.sum(directions[:, :-1] * directions[:, 1:], axis=0)
        * link_flags[:-1]
        * link_flags[1:]
    )
    projected = jnp.sum(directions * link_vectors(updated), axis=0)
    solution = expand(coupling, link_flags * root_half * (projected - rest_length))
    updated = apply_links(updated, directions, solution)
    vectors = link_vectors(updated)
    squared = jnp.sum(vectors * vectors, axis=0)
    target = jnp.sqrt(
        jnp.maximum(2.0 * rest_length * rest_length - squared, 0.25 * rest_length * rest_length)
    )
    solution = expand(coupling, link_flags * root_half * (rest_length - target))
    updated = apply_links(updated, directions, solution)
    return updated


def on_device(positions, velocities, send_list, pair_list, constraint_flags):
    link_flags = constraint_flags.astype(jnp.float32)
    rest_length = link_lengths(positions)
    bead_total = 8 * positions.shape[2] * lax.axis_size(("gx", "gy", "gz"))
    tables = pair_tables(pair_list, positions.shape[2] + send_list.shape[0] + 1)
    forces, potential = local_forces(positions, send_list, pair_list, tables)
    energy_rows = []
    for iteration in range(ITERS):
        half_speed = velocities + 0.5 * time_step * forces
        updated = constrain(positions, positions + time_step * half_speed, rest_length, link_flags)
        half_speed = (updated - positions) / time_step
        forces, potential = local_forces(updated, send_list, pair_list, tables)
        velocities = half_speed + 0.5 * time_step * forces
        positions = updated
        kinetic = 0.5 * jnp.sum(velocities * velocities)
        energy_rows.append(jnp.stack([potential, kinetic]))
    energies = jnp.stack(energy_rows)
    energies = over_axes(energies, ("gx", "gy", "gz"))
    return (positions, velocities, energies / bead_total)


def solution(mesh):
    return jax.shard_map(
        on_device,
        mesh=mesh,
        in_specs=(
            P(None, None, ("runs", "gx", "gy", "gz")),
            P(None, None, ("runs", "gx", "gy", "gz")),
            P(("runs", "gx", "gy", "gz")),
            P(None, ("runs", "gx", "gy", "gz")),
            P(None, ("runs", "gx", "gy", "gz")),
        ),
        out_specs=(
            P(None, None, ("runs", "gx", "gy", "gz")),
            P(None, None, ("runs", "gx", "gy", "gz")),
            P("runs", None),
        ),
        check_vma=False,
    )
```

profile of v0, /device:TPU:65, one launch (start us, length us, event | category | flops | bytes accessed | tf_op | source)
XLA Modules:
  0.0 284.2 jit_solution(5822474635701368043)
XLA Ops:
  4.1 6.3 %collective-permute-start = (f32[3,8,34]{2,1,0:T(8,128)S(1)}, f32[3,8,34]{2,1,0:T(8,128)S(1)}, u32[]{:S(2)}, u32[]{:S(2)}) collective-permute-start(f32[3,8,34]{2,1,0:T(8,128)S(1)} %pad_maximum_fusion.8), channel_id=1, source_target_pairs={{0,14},{2,0},{4,2},{6,4},{8,6},{10,8},{12,10},{14,12},{1,15},{3,1}... | collective-permute-start | bytes 9800 | tf_op jit(solution)/shard_map/ppermute | solution.py:20
  11.5 43.7 %collective-permute-start.1 = (f32[3,8,153]{2,1,0:T(8,128)S(1)}, f32[3,8,153]{2,1,0:T(8,128)S(1)}, u32[]{:S(2)}, u32[]{:S(2)}) collective-permute-start(f32[3,8,153]{2,1,0:T(8,128)S(1)} %pad_maximum_fusion), channel_id=1, source_target_pairs={{0,240},{16,0},{32,16},{48,32},{64,48},{80,64},{96,80},{112,96},{1... | collective-permute-start | bytes 44072 | tf_op jit(solution)/shard_map/ppermute | solution.py:20
  55.2 0.9 collective-permute-done.1
  56.3 4.2 %collective-permute-start.2 = (f32[3,8,18]{2,1,0:T(8,128)S(1)}, f32[3,8,18]{2,1,0:T(8,128)S(1)}, u32[]{:S(2)}, u32[]{:S(2)}) collective-permute-start(f32[3,8,18]{2,1,0:T(8,128)S(1)} %pad_maximum_fusion.9), channel_id=1, source_target_pairs={{0,1},{1,0},{2,3},{3,2},{4,5},{5,4},{6,7},{7,6},{8,9},{9,8},{10,11... | collective-permute-start | bytes 5192 | tf_op jit(solution)/shard_map/ppermute | solution.py:20
  61.5 0.9 fusion.24
  62.4 0.9 fusion.11
  64.1 1.1 fusion.3
  65.2 1.1 fusion.55
  66.6 2.3 collective-permute-start.3
  69.9 1.9 collective-permute-start.4
  71.9 4.4 %collective-permute-done.4 = f32[3,8,153]{2,1,0:T(8,128)S(1)} collective-permute-done((f32[3,8,153]{2,1,0:T(8,128)S(1)}, f32[3,8,153]{2,1,0:T(8,128)S(1)}, u32[]{:S(2)}, u32[]{:S(2)}) %collective-permute-start.4) | collective-permute-done | bytes 14720 | tf_op jit(solution)/shard_map/ppermute | solution.py:20
  76.5 1.9 collective-permute-start.5
  78.7 4.0 %collective-permute-done.5 = f32[3,8,34]{2,1,0:T(8,128)S(1)} collective-permute-done((f32[3,8,34]{2,1,0:T(8,128)S(1)}, f32[3,8,34]{2,1,0:T(8,128)S(1)}, u32[]{:S(2)}, u32[]{:S(2)}) %collective-permute-start.5) | collective-permute-done | bytes 3296 | tf_op jit(solution)/shard_map/ppermute | solution.py:20
  83.2 7.2 %scatter_fusion = f32[3,8,128]{1,0,2:T(4,128)S(1)} fusion(f32[3,8,128]{1,0,2:T(4,128)S(1)} %copy.120, s32[178]{0:T(256)S(1)} %compare_select_fusion, f32[178,3,8]{2,1,0:T(4,128)S(1)} %copy.102), kind=kCustom, calls=%fused_computation.4 | custom fusion | flops 4272 | bytes 51976 | tf_op jit(solution)/shard_map/scatter-add | solution.py:149
  92.1 3.4 %collective-permute-start.6 = (f32[3,8,34]{2,1,0:T(8,128)S(1)}, f32[3,8,34]{2,1,0:T(8,128)S(1)}, u32[]{:S(2)}, u32[]{:S(2)}) collective-permute-start(f32[3,8,34]{2,1,0:T(8,128)S(1)} %pad_maximum_fusion.12), channel_id=1, source_target_pairs={{0,14},{2,0},{4,2},{6,4},{8,6},{10,8},{12,10},{14,12},{1,15},{3,1}... | collective-permute-start | bytes 9800 | tf_op jit(solution)/shard_map/ppermute | solution.py:20
  95.6 1.0 collective-permute-done.6
  96.8 3.4 %collective-permute-start.7 = (f32[3,8,153]{2,1,0:T(8,128)S(1)}, f32[3,8,153]{2,1,0:T(8,128)S(1)}, u32[]{:S(2)}, u32[]{:S(2)}) collective-permute-start(f32[3,8,153]{2,1,0:T(8,128)S(1)} %pad_maximum_fusion.2), channel_id=1, source_target_pairs={{0,240},{16,0},{32,16},{48,32},{64,48},{80,64},{96,80},{112,96},{1... | collective-permute-start | bytes 44072 | tf_op jit(solution)/shard_map/ppermute | solution.py:20
  100.2 1.2 collective-permute-done.7
  101.6 6.3 %collective-permute-start.8 = (f32[3,8,18]{2,1,0:T(8,128)S(1)}, f32[3,8,18]{2,1,0:T(8,128)S(1)}, u32[]{:S(2)}, u32[]{:S(2)}) collective-permute-start(f32[3,8,18]{2,1,0:T(8,128)S(1)} %pad_maximum_fusion.13), channel_id=1, source_target_pairs={{0,1},{1,0},{2,3},{3,2},{4,5},{5,4},{6,7},{7,6},{8,9},{9,8},{10,11... | collective-permute-start | bytes 5192 | tf_op jit(solution)/shard_map/ppermute | solution.py:20
  108.9 0.9 fusion.22
  109.7 0.9 fusion.9
  111.4 1.1 fusion.1
  112.5 1.1 fusion.59
  113.9 2.3 collective-permute-start.9
  117.2 1.9 collective-permute-start.10
  119.2 4.1 %collective-permute-done.10 = f32[3,8,153]{2,1,0:T(8,128)S(1)} collective-permute-done((f32[3,8,153]{2,1,0:T(8,128)S(1)}, f32[3,8,153]{2,1,0:T(8,128)S(1)}, u32[]{:S(2)}, u32[]{:S(2)}) %collective-permute-start.10) | collective-permute-done | bytes 14720 | tf_op jit(solution)/shard_map/ppermute | solution.py:20
  123.5 2.1 collective-permute-start.11
  125.9 3.6 %collective-permute-done.11 = f32[3,8,34]{2,1,0:T(8,128)S(1)} collective-permute-done((f32[3,8,34]{2,1,0:T(8,128)S(1)}, f32[3,8,34]{2,1,0:T(8,128)S(1)}, u32[]{:S(2)}, u32[]{:S(2)}) %collective-permute-start.11) | collective-permute-done | bytes 3296 | tf_op jit(solution)/shard_map/ppermute | solution.py:20
  129.9 7.2 %scatter_fusion.1 = f32[3,8,128]{1,0,2:T(4,128)S(1)} fusion(f32[3,8,128]{1,0,2:T(4,128)S(1)} %copy.121, s32[178]{0:T(256)S(1)} %compare_select_fusion, f32[178,3,8]{2,1,0:T(4,128)S(1)} %copy.107), kind=kCustom, calls=%fused_computation.5 | custom fusion | flops 4272 | bytes 51976 | tf_op jit(solution)/shard_map/scatter-add | solution.py:149
  138.9 3.4 %collective-permute-start.12 = (f32[3,8,34]{2,1,0:T(8,128)S(1)}, f32[3,8,34]{2,1,0:T(8,128)S(1)}, u32[]{:S(2)}, u32[]{:S(2)}) collective-permute-start(f32[3,8,34]{2,1,0:T(8,128)S(1)} %pad_maximum_fusion.16), channel_id=1, source_target_pairs={{0,14},{2,0},{4,2},{6,4},{8,6},{10,8},{12,10},{14,12},{1,15},{3,1}... | collective-permute-start | bytes 9800 | tf_op jit(solution)/shard_map/ppermute | solution.py:20
  142.3 1.0 collective-permute-done.12
  143.6 3.4 %collective-permute-start.13 = (f32[3,8,153]{2,1,0:T(8,128)S(1)}, f32[3,8,153]{2,1,0:T(8,128)S(1)}, u32[]{:S(2)}, u32[]{:S(2)}) collective-permute-start(f32[3,8,153]{2,1,0:T(8,128)S(1)} %pad_maximum_fusion.4), channel_id=1, source_target_pairs={{0,240},{16,0},{32,16},{48,32},{64,48},{80,64},{96,80},{112,96},{1... | collective-permute-start | bytes 44072 | tf_op jit(solution)/shard_map/ppermute | solution.py:20
  147.0 1.2 collective-permute-done.13
  148.3 6.3 %collective-permute-start.14 = (f32[3,8,18]{2,1,0:T(8,128)S(1)}, f32[3,8,18]{2,1,0:T(8,128)S(1)}, u32[]{:S(2)}, u32[]{:S(2)}) collective-permute-start(f32[3,8,18]{2,1,0:T(8,128)S(1)} %pad_maximum_fusion.17), channel_id=1, source_target_pairs={{0,1},{1,0},{2,3},{3,2},{4,5},{5,4},{6,7},{7,6},{8,9},{9,8},{10,11... | collective-permute-start | bytes 5192 | tf_op jit(solution)/shard_map/ppermute | solution.py:20
  155.6 0.9 fusion.20
  156.5 0.9 fusion.7
  158.2 1.1 fusion
  159.2 1.1 fusion.61
  160.6 2.3 collective-permute-start.15
  164.0 1.9 collective-permute-start.16
  165.9 4.1 %collective-permute-done.16 = f32[3,8,153]{2,1,0:T(8,128)S(1)} collective-permute-done((f32[3,8,153]{2,1,0:T(8,128)S(1)}, f32[3,8,153]{2,1,0:T(8,128)S(1)}, u32[]{:S(2)}, u32[]{:S(2)}) %collective-permute-start.16) | collective-permute-done | bytes 14720 | tf_op jit(solution)/shard_map/ppermute | solution.py:20
  170.2 1.9 collective-permute-start.17
  172.4 3.7 %collective-permute-done.17 = f32[3,8,34]{2,1,0:T(8,128)S(1)} collective-permute-done((f32[3,8,34]{2,1,0:T(8,128)S(1)}, f32[3,8,34]{2,1,0:T(8,128)S(1)}, u32[]{:S(2)}, u32[]{:S(2)}) %collective-permute-start.17) | collective-permute-done | bytes 3296 | tf_op jit(solution)/shard_map/ppermute | solution.py:20
  176.6 7.2 %scatter_fusion.2 = f32[3,8,128]{1,0,2:T(4,128)S(1)} fusion(f32[3,8,128]{1,0,2:T(4,128)S(1)} %copy.122, s32[178]{0:T(256)S(1)} %compare_select_fusion, f32[178,3,8]{2,1,0:T(4,128)S(1)} %copy.112), kind=kCustom, calls=%fused_computation.6 | custom fusion | flops 4272 | bytes 51976 | tf_op jit(solution)/shard_map/scatter-add | solution.py:149
  186.2 3.4 %collective-permute-start.18 = (f32[3,8,34]{2,1,0:T(8,128)S(1)}, f32[3,8,34]{2,1,0:T(8,128)S(1)}, u32[]{:S(2)}, u32[]{:S(2)}) collective-permute-start(f32[3,8,34]{2,1,0:T(8,128)S(1)} %pad_maximum_fusion.20), channel_id=1, source_target_pairs={{0,14},{2,0},{4,2},{6,4},{8,6},{10,8},{12,10},{14,12},{1,15},{3,1}... | collective-permute-start | bytes 9800 | tf_op jit(solution)/shard_map/ppermute | solution.py:20
  189.7 1.0 collective-permute-done.18
  190.9 3.4 %collective-permute-start.19 = (f32[3,8,153]{2,1,0:T(8,128)S(1)}, f32[3,8,153]{2,1,0:T(8,128)S(1)}, u32[]{:S(2)}, u32[]{:S(2)}) collective-permute-start(f32[3,8,153]{2,1,0:T(8,128)S(1)} %pad_maximum_fusion.6), channel_id=1, source_target_pairs={{0,240},{16,0},{32,16},{48,32},{64,48},{80,64},{96,80},{112,96},{1... | collective-permute-start | bytes 44072 | tf_op jit(solution)/shard_map/ppermute | solution.py:20
  194.3 1.2 collective-permute-done.19
  195.7 6.5 %collective-permute-start.20 = (f32[3,8,18]{2,1,0:T(8,128)S(1)}, f32[3,8,18]{2,1,0:T(8,128)S(1)}, u32[]{:S(2)}, u32[]{:S(2)}) collective-permute-start(f32[3,8,18]{2,1,0:T(8,128)S(1)} %pad_maximum_fusion.21), channel_id=1, source_target_pairs={{0,1},{1,0},{2,3},{3,2},{4,5},{5,4},{6,7},{7,6},{8,9},{9,8},{10,11... | collective-permute-start | bytes 5192 | tf_op jit(solution)/shard_map/ppermute | solution.py:20
  203.0 0.9 fusion.18
  203.8 0.9 fusion.5
  204.9 1.1 fusion.66
  206.4 1.1 fusion.2
  207.5 1.1 fusion.57
  208.9 2.3 collective-permute-start.21
  212.2 1.9 collective-permute-start.22
  216.6 1.6 collective-permute-done.22
  218.4 1.9 collective-permute-start.23
  221.4 3.0 %collective-permute-done.23 = f32[3,8,34]{2,1,0:T(8,128)S(1)} collective-permute-done((f32[3,8,34]{2,1,0:T(8,128)S(1)}, f32[3,8,34]{2,1,0:T(8,128)S(1)}, u32[]{:S(2)}, u32[]{:S(2)}) %collective-permute-start.23) | collective-permute-done | bytes 3296 | tf_op jit(solution)/shard_map/ppermute | solution.py:20
  224.9 7.2 %scatter_fusion.3 = f32[3,8,128]{1,0,2:T(4,128)S(1)} fusion(f32[3,8,128]{1,0,2:T(4,128)S(1)} %copy.123, s32[178]{0:T(256)S(1)} %compare_select_fusion, f32[178,3,8]{2,1,0:T(4,128)S(1)} %copy.117), kind=kCustom, calls=%fused_computation.7 | custom fusion | flops 4272 | bytes 51976 | tf_op jit(solution)/shard_map/scatter-add | solution.py:149
  232.1 1.2 multiply_reduce_fusion
  234.1 21.7 %psum.21 = f32[3,2]{1,0:T(4,128)S(1)} all-reduce(f32[3,2]{1,0:T(4,128)S(1)} %pad_maximum_fusion.24), channel_id=1, replica_groups=mesh['runs'=2,'gx'=16,'gy'=8,'gz'=2] {'gx'}, use_global_device_ids=true, to_apply=%region_34.36 | all-reduce | flops 6 | bytes 48 | tf_op jit(solution)/shard_map/psum | solution.py:25
  255.8 11.9 %psum.22 = f32[3,2]{1,0:T(4,128)S(1)} all-reduce(f32[3,2]{1,0:T(4,128)S(1)} %psum.21), channel_id=1, replica_groups=mesh['runs'=2,'gx'=16,'gy'=8,'gz'=2] {'gy'}, use_global_device_ids=true, to_apply=%region_35.37 | all-reduce | flops 6 | bytes 48 | tf_op jit(solution)/shard_map/psum | solution.py:25
  267.8 15.8 %psum.23 = f32[3,2]{1,0:T(4,128)S(1)} all-reduce(f32[3,2]{1,0:T(4,128)S(1)} %psum.22), channel_id=1, replica_groups=mesh['runs'=2,'gx'=16,'gy'=8,'gz'=2] {'gz'}, use_global_device_ids=true, to_apply=%region_36.38 | all-reduce | flops 6 | bytes 48 | tf_op jit(solution)/shard_map/psum | solution.py:25
  (264 shorter events, 27.9 us)
Async XLA Ops:
  2.0 8.5 %copy-start.4 = (s32[2,1792]{1,0:T(2,128)S(1)}, s32[2,1792]{1,0:T(2,128)}, u32[]{:S(2)}) copy-start(s32[2,1792]{1,0:T(2,128)} %param.14) | copy-start | bytes 43012
  3.9 57.6 %copy-start.3 = (f32[3,178]{1,0:T(4,128)S(1)}, f32[3,178]{1,0:T(4,128)}, u32[]{:S(2)}) copy-start(f32[3,178]{1,0:T(4,128)} %constant.57.clone) | copy-start | bytes 6412
  3.9 57.7 %copy-start = (f32[3,8,128]{2,1,0:T(8,128)S(1)}, f32[3,8,128]{2,1,0:T(8,128)}, u32[]{:S(2)}) copy-start(f32[3,8,128]{2,1,0:T(8,128)} %param.11) | copy-start | bytes 36868
  4.1 7.1 %collective-permute-start = (f32[3,8,34]{2,1,0:T(8,128)S(1)}, f32[3,8,34]{2,1,0:T(8,128)S(1)}, u32[]{:S(2)}, u32[]{:S(2)}) collective-permute-start(f32[3,8,34]{2,1,0:T(8,128)S(1)} %pad_maximum_fusion.8), channel_id=1, source_target_pairs={{0,14},{2,0},{4,2},{6,4},{8,6},{10,8},{12,10},{14,12},{1,15},{3,1}... | collective-permute-start | bytes 9800 | tf_op jit(solution)/shard_map/ppermute | solution.py:20
  11.5 44.7 %collective-permute-start.1 = (f32[3,8,153]{2,1,0:T(8,128)S(1)}, f32[3,8,153]{2,1,0:T(8,128)S(1)}, u32[]{:S(2)}, u32[]{:S(2)}) collective-permute-start(f32[3,8,153]{2,1,0:T(8,128)S(1)} %pad_maximum_fusion), channel_id=1, source_target_pairs={{0,240},{16,0},{32,16},{48,32},{64,48},{80,64},{96,80},{112,96},{1... | collective-permute-start | bytes 44072 | tf_op jit(solution)/shard_map/ppermute | solution.py:20
  56.3 5.1 %collective-permute-start.2 = (f32[3,8,18]{2,1,0:T(8,128)S(1)}, f32[3,8,18]{2,1,0:T(8,128)S(1)}, u32[]{:S(2)}, u32[]{:S(2)}) collective-permute-start(f32[3,8,18]{2,1,0:T(8,128)S(1)} %pad_maximum_fusion.9), channel_id=1, source_target_pairs={{0,1},{1,0},{2,3},{3,2},{4,5},{5,4},{6,7},{7,6},{8,9},{9,8},{10,11... | collective-permute-start | bytes 5192 | tf_op jit(solution)/shard_map/ppermute | solution.py:20
  65.2 13.2 %copy-start.1 = (s32[7,128]{1,0:T(8,128)S(1)}, s32[7,128]{1,0:T(8,128)}, u32[]{:S(2)}) copy-start(s32[7,128]{1,0:T(8,128)} %param.15) | copy-start | bytes 10756
  66.6 3.1 %collective-permute-start.3 = (f32[3,8,18]{2,1,0:T(8,128)S(1)}, f32[3,8,18]{2,1,0:T(8,128)S(1)}, u32[]{:S(2)}, u32[]{:S(2)}) collective-permute-start(f32[3,8,18]{2,1,0:T(8,128)S(1)} %pad_maximum_fusion.10), channel_id=1, source_target_pairs={{0,1},{1,0},{2,3},{3,2},{4,5},{5,4},{6,7},{7,6},{8,9},{9,8},{10,11... | collective-permute-start | bytes 5192 | tf_op jit(solution)/shard_map/ppermute | solution.py:20
  69.9 6.4 %collective-permute-start.4 = (f32[3,8,153]{2,1,0:T(8,128)S(1)}, f32[3,8,153]{2,1,0:T(8,128)S(1)}, u32[]{:S(2)}, u32[]{:S(2)}) collective-permute-start(f32[3,8,153]{2,1,0:T(8,128)S(1)} %pad_maximum_fusion.1), channel_id=1, source_target_pairs={{0,16},{16,32},{32,48},{48,64},{64,80},{80,96},{96,112},{112,128},... | collective-permute-start | bytes 44072 | tf_op jit(solution)/shard_map/ppermute | solution.py:20
  76.5 6.2 %collective-permute-start.5 = (f32[3,8,34]{2,1,0:T(8,128)S(1)}, f32[3,8,34]{2,1,0:T(8,128)S(1)}, u32[]{:S(2)}, u32[]{:S(2)}) collective-permute-start(f32[3,8,34]{2,1,0:T(8,128)S(1)} %pad_maximum_fusion.11), channel_id=1, source_target_pairs={{0,2},{2,4},{4,6},{6,8},{8,10},{10,12},{12,14},{14,0},{1,3},{3,5},... | collective-permute-start | bytes 9800 | tf_op jit(solution)/shard_map/ppermute | solution.py:20
  78.7 11.7 %copy-start.5 = (f32[3,8,128]{2,1,0:T(8,128)S(1)}, f32[3,8,128]{2,1,0:T(8,128)}, u32[]{:S(2)}) copy-start(f32[3,8,128]{2,1,0:T(8,128)} %param.12) | copy-start | bytes 36868
  92.1 4.5 %collective-permute-start.6 = (f32[3,8,34]{2,1,0:T(8,128)S(1)}, f32[3,8,34]{2,1,0:T(8,128)S(1)}, u32[]{:S(2)}, u32[]{:S(2)}) collective-permute-start(f32[3,8,34]{2,1,0:T(8,128)S(1)} %pad_maximum_fusion.12), channel_id=1, source_target_pairs={{0,14},{2,0},{4,2},{6,4},{8,6},{10,8},{12,10},{14,12},{1,15},{3,1}... | collective-permute-start | bytes 9800 | tf_op jit(solution)/shard_map/ppermute | solution.py:20
  96.8 4.6 %collective-permute-start.7 = (f32[3,8,153]{2,1,0:T(8,128)S(1)}, f32[3,8,153]{2,1,0:T(8,128)S(1)}, u32[]{:S(2)}, u32[]{:S(2)}) collective-permute-start(f32[3,8,153]{2,1,0:T(8,128)S(1)} %pad_maximum_fusion.2), channel_id=1, source_target_pairs={{0,240},{16,0},{32,16},{48,32},{64,48},{80,64},{96,80},{112,96},{1... | collective-permute-start | bytes 44072 | tf_op jit(solution)/shard_map/ppermute | solution.py:20
  101.6 7.1 %collective-permute-start.8 = (f32[3,8,18]{2,1,0:T(8,128)S(1)}, f32[3,8,18]{2,1,0:T(8,128)S(1)}, u32[]{:S(2)}, u32[]{:S(2)}) collective-permute-start(f32[3,8,18]{2,1,0:T(8,128)S(1)} %pad_maximum_fusion.13), channel_id=1, source_target_pairs={{0,1},{1,0},{2,3},{3,2},{4,5},{5,4},{6,7},{7,6},{8,9},{9,8},{10,11... | collective-permute-start | bytes 5192 | tf_op jit(solution)/shard_map/ppermute | solution.py:20
  113.9 3.1 %collective-permute-start.9 = (f32[3,8,18]{2,1,0:T(8,128)S(1)}, f32[3,8,18]{2,1,0:T(8,128)S(1)}, u32[]{:S(2)}, u32[]{:S(2)}) collective-permute-start(f32[3,8,18]{2,1,0:T(8,128)S(1)} %pad_maximum_fusion.14), channel_id=1, source_target_pairs={{0,1},{1,0},{2,3},{3,2},{4,5},{5,4},{6,7},{7,6},{8,9},{9,8},{10,11... | collective-permute-start | bytes 5192 | tf_op jit(solution)/shard_map/ppermute | solution.py:20
  117.2 6.1 %collective-permute-start.10 = (f32[3,8,153]{2,1,0:T(8,128)S(1)}, f32[3,8,153]{2,1,0:T(8,128)S(1)}, u32[]{:S(2)}, u32[]{:S(2)}) collective-permute-start(f32[3,8,153]{2,1,0:T(8,128)S(1)} %pad_maximum_fusion.3), channel_id=1, source_target_pairs={{0,16},{16,32},{32,48},{48,64},{64,80},{80,96},{96,112},{112,128},... | collective-permute-start | bytes 44072 | tf_op jit(solution)/shard_map/ppermute | solution.py:20
  123.5 6.0 %collective-permute-start.11 = (f32[3,8,34]{2,1,0:T(8,128)S(1)}, f32[3,8,34]{2,1,0:T(8,128)S(1)}, u32[]{:S(2)}, u32[]{:S(2)}) collective-permute-start(f32[3,8,34]{2,1,0:T(8,128)S(1)} %pad_maximum_fusion.15), channel_id=1, source_target_pairs={{0,2},{2,4},{4,6},{6,8},{8,10},{10,12},{12,14},{14,0},{1,3},{3,5},... | collective-permute-start | bytes 9800 | tf_op jit(solution)/shard_map/ppermute | solution.py:20
  138.9 4.5 %collective-permute-start.12 = (f32[3,8,34]{2,1,0:T(8,128)S(1)}, f32[3,8,34]{2,1,0:T(8,128)S(1)}, u32[]{:S(2)}, u32[]{:S(2)}) collective-permute-start(f32[3,8,34]{2,1,0:T(8,128)S(1)} %pad_maximum_fusion.16), channel_id=1, source_target_pairs={{0,14},{2,0},{4,2},{6,4},{8,6},{10,8},{12,10},{14,12},{1,15},{3,1}... | collective-permute-start | bytes 9800 | tf_op jit(solution)/shard_map/ppermute | solution.py:20
  143.6 4.6 %collective-permute-start.13 = (f32[3,8,153]{2,1,0:T(8,128)S(1)}, f32[3,8,153]{2,1,0:T(8,128)S(1)}, u32[]{:S(2)}, u32[]{:S(2)}) collective-permute-start(f32[3,8,153]{2,1,0:T(8,128)S(1)} %pad_maximum_fusion.4), channel_id=1, source_target_pairs={{0,240},{16,0},{32,16},{48,32},{64,48},{80,64},{96,80},{112,96},{1... | collective-permute-start | bytes 44072 | tf_op jit(solution)/shard_map/ppermute | solution.py:20
  148.3 7.1 %collective-permute-start.14 = (f32[3,8,18]{2,1,0:T(8,128)S(1)}, f32[3,8,18]{2,1,0:T(8,128)S(1)}, u32[]{:S(2)}, u32[]{:S(2)}) collective-permute-start(f32[3,8,18]{2,1,0:T(8,128)S(1)} %pad_maximum_fusion.17), channel_id=1, source_target_pairs={{0,1},{1,0},{2,3},{3,2},{4,5},{5,4},{6,7},{7,6},{8,9},{9,8},{10,11... | collective-permute-start | bytes 5192 | tf_op jit(solution)/shard_map/ppermute | solution.py:20
  160.6 3.1 %collective-permute-start.15 = (f32[3,8,18]{2,1,0:T(8,128)S(1)}, f32[3,8,18]{2,1,0:T(8,128)S(1)}, u32[]{:S(2)}, u32[]{:S(2)}) collective-permute-start(f32[3,8,18]{2,1,0:T(8,128)S(1)} %pad_maximum_fusion.18), channel_id=1, source_target_pairs={{0,1},{1,0},{2,3},{3,2},{4,5},{5,4},{6,7},{7,6},{8,9},{9,8},{10,11... | collective-permute-start | bytes 5192 | tf_op jit(solution)/shard_map/ppermute | solution.py:20
  164.0 6.1 %collective-permute-start.16 = (f32[3,8,153]{2,1,0:T(8,128)S(1)}, f32[3,8,153]{2,1,0:T(8,128)S(1)}, u32[]{:S(2)}, u32[]{:S(2)}) collective-permute-start(f32[3,8,153]{2,1,0:T(8,128)S(1)} %pad_maximum_fusion.5), channel_id=1, source_target_pairs={{0,16},{16,32},{32,48},{48,64},{64,80},{80,96},{96,112},{112,128},... | collective-permute-start | bytes 44072 | tf_op jit(solution)/shard_map/ppermute | solution.py:20
  170.2 6.0 %collective-permute-start.17 = (f32[3,8,34]{2,1,0:T(8,128)S(1)}, f32[3,8,34]{2,1,0:T(8,128)S(1)}, u32[]{:S(2)}, u32[]{:S(2)}) collective-permute-start(f32[3,8,34]{2,1,0:T(8,128)S(1)} %pad_maximum_fusion.19), channel_id=1, source_target_pairs={{0,2},{2,4},{4,6},{6,8},{8,10},{10,12},{12,14},{14,0},{1,3},{3,5},... | collective-permute-start | bytes 9800 | tf_op jit(solution)/shard_map/ppermute | solution.py:20
  184.8 47.3 %copy-start.2 = (f32[3,8,128]{2,1,0:T(8,128)}, f32[3,8,128]{2,1,0:T(8,128)S(1)}, u32[]{:S(2)}) copy-start(f32[3,8,128]{2,1,0:T(8,128)S(1)} %pad_add_fusion) | copy-start | bytes 36868
  186.2 4.5 %collective-permute-start.18 = (f32[3,8,34]{2,1,0:T(8,128)S(1)}, f32[3,8,34]{2,1,0:T(8,128)S(1)}, u32[]{:S(2)}, u32[]{:S(2)}) collective-permute-start(f32[3,8,34]{2,1,0:T(8,128)S(1)} %pad_maximum_fusion.20), channel_id=1, source_target_pairs={{0,14},{2,0},{4,2},{6,4},{8,6},{10,8},{12,10},{14,12},{1,15},{3,1}... | collective-permute-start | bytes 9800 | tf_op jit(solution)/shard_map/ppermute | solution.py:20
  190.9 4.6 %collective-permute-start.19 = (f32[3,8,153]{2,1,0:T(8,128)S(1)}, f32[3,8,153]{2,1,0:T(8,128)S(1)}, u32[]{:S(2)}, u32[]{:S(2)}) collective-permute-start(f32[3,8,153]{2,1,0:T(8,128)S(1)} %pad_maximum_fusion.6), channel_id=1, source_target_pairs={{0,240},{16,0},{32,16},{48,32},{64,48},{80,64},{96,80},{112,96},{1... | collective-permute-start | bytes 44072 | tf_op jit(solution)/shard_map/ppermute | solution.py:20
  195.7 7.1 %collective-permute-start.20 = (f32[3,8,18]{2,1,0:T(8,128)S(1)}, f32[3,8,18]{2,1,0:T(8,128)S(1)}, u32[]{:S(2)}, u32[]{:S(2)}) collective-permute-start(f32[3,8,18]{2,1,0:T(8,128)S(1)} %pad_maximum_fusion.21), channel_id=1, source_target_pairs={{0,1},{1,0},{2,3},{3,2},{4,5},{5,4},{6,7},{7,6},{8,9},{9,8},{10,11... | collective-permute-start | bytes 5192 | tf_op jit(solution)/shard_map/ppermute | solution.py:20
  208.9 3.1 %collective-permute-start.21 = (f32[3,8,18]{2,1,0:T(8,128)S(1)}, f32[3,8,18]{2,1,0:T(8,128)S(1)}, u32[]{:S(2)}, u32[]{:S(2)}) collective-permute-start(f32[3,8,18]{2,1,0:T(8,128)S(1)} %pad_maximum_fusion.22), channel_id=1, source_target_pairs={{0,1},{1,0},{2,3},{3,2},{4,5},{5,4},{6,7},{7,6},{8,9},{9,8},{10,11... | collective-permute-start | bytes 5192 | tf_op jit(solution)/shard_map/ppermute | solution.py:20
  212.2 6.1 %collective-permute-start.22 = (f32[3,8,153]{2,1,0:T(8,128)S(1)}, f32[3,8,153]{2,1,0:T(8,128)S(1)}, u32[]{:S(2)}, u32[]{:S(2)}) collective-permute-start(f32[3,8,153]{2,1,0:T(8,128)S(1)} %pad_maximum_fusion.7), channel_id=1, source_target_pairs={{0,16},{16,32},{32,48},{48,64},{64,80},{80,96},{96,112},{112,128},... | collective-permute-start | bytes 44072 | tf_op jit(solution)/shard_map/ppermute | solution.py:20
  218.4 6.0 %collective-permute-start.23 = (f32[3,8,34]{2,1,0:T(8,128)S(1)}, f32[3,8,34]{2,1,0:T(8,128)S(1)}, u32[]{:S(2)}, u32[]{:S(2)}) collective-permute-start(f32[3,8,34]{2,1,0:T(8,128)S(1)} %pad_maximum_fusion.23), channel_id=1, source_target_pairs={{0,2},{2,4},{4,6},{6,8},{8,10},{10,12},{12,14},{14,0},{1,3},{3,5},... | collective-permute-start | bytes 9800 | tf_op jit(solution)/shard_map/ppermute | solution.py:20
where the time goes:
time: 285 us; the launch traced here: 284 us
  starting transfers between devices  119 us (42%)
  blocking collectives  49.5 us (17%)
  waiting for transfers between devices  42.6 us (15%)
  other arithmetic  38.8 us (14%)
  matrix products  15.5 us (5%)
  local copies, waits for them, and re-layouts  13.6 us (5%)
  between operations  5.59 us (2%)
    ppermute x24, starting transfers between devices, from_behind(): lax.ppermute(value, axis, [(i, (i + by) % count) for i in range(count)])  119 us
    psum x3, blocking collectives, over_axes(): value = lax.psum(value, axis)  49.5 us
    ppermute x24, waiting for transfers between devices, from_behind(): lax.ppermute(value, axis, [(i, (i + by) % count) for i in range(count)])  42.6 us
    scatter-add x4, other arithmetic, local_forces(): home_forces = forces[:, :, :cluster_count].at[:, :, send_list].add(returned)  28.6 us
  transfers between devices with their start and end apart: 24, of which 24 were waited for; matrix products, arithmetic and copies ran while one was open for 1% of the time, Pallas kernels for 0%

commit v1 on v0

--- a/solution.py
+++ b/solution.py
@@ -22,7 +22,7 @@
 
 def over_axes(value, axes):
     for axis in axes:
-        value = lax.psum(value, axis)
+        value = jnp.sum(lax.all_gather(value, axis), axis=0)
     return value
 
 

time: 285 us -> 283 us (level)
    psum x3 -> x0, blocking collectives: 49.5 us -> none  [over_axes(): value = lax.psum(value, axis)]
    all_gather x0 -> x3, blocking collectives: none -> 46.9 us  [over_axes(): value = jnp.sum(lax.all_gather(value, axis), axis=0)]
where the time goes in v1:
time: 283 us; the launch traced here: 282 us
  starting transfers between devices  119 us (42%)
  blocking collectives  46.9 us (17%)
  waiting for transfers between devices  42.6 us (15%)
  other arithmetic  39.4 us (14%)
  matrix products  15.5 us (5%)
  local copies, waits for them, and re-layouts  13 us (5%)
  between operations  5.59 us (2%)
    ppermute x24, starting transfers between devices, from_behind(): lax.ppermute(value, axis, [(i, (i + by) % count) for i in range(count)])  119 us
    all_gather x3, blocking collectives, over_axes(): value = jnp.sum(lax.all_gather(value, axis), axis=0)  46.9 us
    ppermute x24, waiting for transfers between devices, from_behind(): lax.ppermute(value, axis, [(i, (i + by) % count) for i in range(count)])  42.6 us
    scatter-add x4, other arithmetic, local_forces(): home_forces = forces[:, :, :cluster_count].at[:, :, send_list].add(returned)  28.6 us
  transfers between devices with their start and end apart: 24, of which 24 were waited for; matrix products, arithmetic and copies ran while one was open for 1% of the time, Pallas kernels for 0%

profile of v1, /device:TPU:65, one launch (start us, length us, event | category | flops | bytes accessed | tf_op | source)
XLA Modules:
  0.0 281.8 jit_solution(11140984390668547287)
XLA Ops:
  4.1 6.3 %collective-permute-start = (f32[3,8,34]{2,1,0:T(8,128)S(1)}, f32[3,8,34]{2,1,0:T(8,128)S(1)}, u32[]{:S(2)}, u32[]{:S(2)}) collective-permute-start(f32[3,8,34]{2,1,0:T(8,128)S(1)} %pad_maximum_fusion.8), channel_id=1, source_target_pairs={{0,14},{2,0},{4,2},{6,4},{8,6},{10,8},{12,10},{14,12},{1,15},{3,1}... | collective-permute-start | bytes 9800 | tf_op jit(solution)/shard_map/ppermute | solution.py:20
  11.5 43.7 %collective-permute-start.1 = (f32[3,8,153]{2,1,0:T(8,128)S(1)}, f32[3,8,153]{2,1,0:T(8,128)S(1)}, u32[]{:S(2)}, u32[]{:S(2)}) collective-permute-start(f32[3,8,153]{2,1,0:T(8,128)S(1)} %pad_maximum_fusion), channel_id=1, source_target_pairs={{0,240},{16,0},{32,16},{48,32},{64,48},{80,64},{96,80},{112,96},{1... | collective-permute-start | bytes 44072 | tf_op jit(solution)/shard_map/ppermute | solution.py:20
  55.2 0.9 collective-permute-done.1
  56.3 4.2 %collective-permute-start.2 = (f32[3,8,18]{2,1,0:T(8,128)S(1)}, f32[3,8,18]{2,1,0:T(8,128)S(1)}, u32[]{:S(2)}, u32[]{:S(2)}) collective-permute-start(f32[3,8,18]{2,1,0:T(8,128)S(1)} %pad_maximum_fusion.9), channel_id=1, source_target_pairs={{0,1},{1,0},{2,3},{3,2},{4,5},{5,4},{6,7},{7,6},{8,9},{9,8},{10,11... | collective-permute-start | bytes 5192 | tf_op jit(solution)/shard_map/ppermute | solution.py:20
  61.5 0.9 fusion.24
  62.4 0.9 fusion.11
  64.1 1.1 fusion.3
  65.2 1.1 fusion.55
  66.6 2.3 collective-permute-start.3
  69.9 1.9 collective-permute-start.4
  71.9 4.4 %collective-permute-done.4 = f32[3,8,153]{2,1,0:T(8,128)S(1)} collective-permute-done((f32[3,8,153]{2,1,0:T(8,128)S(1)}, f32[3,8,153]{2,1,0:T(8,128)S(1)}, u32[]{:S(2)}, u32[]{:S(2)}) %collective-permute-start.4) | collective-permute-done | bytes 14720 | tf_op jit(solution)/shard_map/ppermute | solution.py:20
  76.5 1.9 collective-permute-start.5
  78.7 4.0 %collective-permute-done.5 = f32[3,8,34]{2,1,0:T(8,128)S(1)} collective-permute-done((f32[3,8,34]{2,1,0:T(8,128)S(1)}, f32[3,8,34]{2,1,0:T(8,128)S(1)}, u32[]{:S(2)}, u32[]{:S(2)}) %collective-permute-start.5) | collective-permute-done | bytes 3296 | tf_op jit(solution)/shard_map/ppermute | solution.py:20
  83.2 7.2 %scatter_fusion = f32[3,8,128]{1,0,2:T(4,128)S(1)} fusion(f32[3,8,128]{1,0,2:T(4,128)S(1)} %copy.120, s32[178]{0:T(256)S(1)} %compare_select_fusion, f32[178,3,8]{2,1,0:T(4,128)S(1)} %copy.102), kind=kCustom, calls=%fused_computation.4 | custom fusion | flops 4272 | bytes 51976 | tf_op jit(solution)/shard_map/scatter-add | solution.py:149
  92.1 3.4 %collective-permute-start.6 = (f32[3,8,34]{2,1,0:T(8,128)S(1)}, f32[3,8,34]{2,1,0:T(8,128)S(1)}, u32[]{:S(2)}, u32[]{:S(2)}) collective-permute-start(f32[3,8,34]{2,1,0:T(8,128)S(1)} %pad_maximum_fusion.12), channel_id=1, source_target_pairs={{0,14},{2,0},{4,2},{6,4},{8,6},{10,8},{12,10},{14,12},{1,15},{3,1}... | collective-permute-start | bytes 9800 | tf_op jit(solution)/shard_map/ppermute | solution.py:20
  95.6 1.0 collective-permute-done.6
  96.8 3.4 %collective-permute-start.7 = (f32[3,8,153]{2,1,0:T(8,128)S(1)}, f32[3,8,153]{2,1,0:T(8,128)S(1)}, u32[]{:S(2)}, u32[]{:S(2)}) collective-permute-start(f32[3,8,153]{2,1,0:T(8,128)S(1)} %pad_maximum_fusion.2), channel_id=1, source_target_pairs={{0,240},{16,0},{32,16},{48,32},{64,48},{80,64},{96,80},{112,96},{1... | collective-permute-start | bytes 44072 | tf_op jit(solution)/shard_map/ppermute | solution.py:20
  100.2 1.2 collective-permute-done.7
  101.6 6.3 %collective-permute-start.8 = (f32[3,8,18]{2,1,0:T(8,128)S(1)}, f32[3,8,18]{2,1,0:T(8,128)S(1)}, u32[]{:S(2)}, u32[]{:S(2)}) collective-permute-start(f32[3,8,18]{2,1,0:T(8,128)S(1)} %pad_maximum_fusion.13), channel_id=1, source_target_pairs={{0,1},{1,0},{2,3},{3,2},{4,5},{5,4},{6,7},{7,6},{8,9},{9,8},{10,11... | collective-permute-start | bytes 5192 | tf_op jit(solution)/shard_map/ppermute | solution.py:20
  108.9 0.9 fusion.22
  109.8 0.9 fusion.9
  111.4 1.1 fusion.1
  112.5 1.1 fusion.59
  113.9 2.3 collective-permute-start.9
  117.2 1.9 collective-permute-start.10
  119.2 4.1 %collective-permute-done.10 = f32[3,8,153]{2,1,0:T(8,128)S(1)} collective-permute-done((f32[3,8,153]{2,1,0:T(8,128)S(1)}, f32[3,8,153]{2,1,0:T(8,128)S(1)}, u32[]{:S(2)}, u32[]{:S(2)}) %collective-permute-start.10) | collective-permute-done | bytes 14720 | tf_op jit(solution)/shard_map/ppermute | solution.py:20
  123.5 2.1 collective-permute-start.11
  125.9 3.6 %collective-permute-done.11 = f32[3,8,34]{2,1,0:T(8,128)S(1)} collective-permute-done((f32[3,8,34]{2,1,0:T(8,128)S(1)}, f32[3,8,34]{2,1,0:T(8,128)S(1)}, u32[]{:S(2)}, u32[]{:S(2)}) %collective-permute-start.11) | collective-permute-done | bytes 3296 | tf_op jit(solution)/shard_map/ppermute | solution.py:20
  129.9 7.2 %scatter_fusion.1 = f32[3,8,128]{1,0,2:T(4,128)S(1)} fusion(f32[3,8,128]{1,0,2:T(4,128)S(1)} %copy.121, s32[178]{0:T(256)S(1)} %compare_select_fusion, f32[178,3,8]{2,1,0:T(4,128)S(1)} %copy.107), kind=kCustom, calls=%fused_computation.5 | custom fusion | flops 4272 | bytes 51976 | tf_op jit(solution)/shard_map/scatter-add | solution.py:149
  138.9 3.4 %collective-permute-start.12 = (f32[3,8,34]{2,1,0:T(8,128)S(1)}, f32[3,8,34]{2,1,0:T(8,128)S(1)}, u32[]{:S(2)}, u32[]{:S(2)}) collective-permute-start(f32[3,8,34]{2,1,0:T(8,128)S(1)} %pad_maximum_fusion.16), channel_id=1, source_target_pairs={{0,14},{2,0},{4,2},{6,4},{8,6},{10,8},{12,10},{14,12},{1,15},{3,1}... | collective-permute-start | bytes 9800 | tf_op jit(solution)/shard_map/ppermute | solution.py:20
  142.3 1.0 collective-permute-done.12
  143.6 3.4 %collective-permute-start.13 = (f32[3,8,153]{2,1,0:T(8,128)S(1)}, f32[3,8,153]{2,1,0:T(8,128)S(1)}, u32[]{:S(2)}, u32[]{:S(2)}) collective-permute-start(f32[3,8,153]{2,1,0:T(8,128)S(1)} %pad_maximum_fusion.4), channel_id=1, source_target_pairs={{0,240},{16,0},{32,16},{48,32},{64,48},{80,64},{96,80},{112,96},{1... | collective-permute-start | bytes 44072 | tf_op jit(solution)/shard_map/ppermute | solution.py:20
  147.0 1.2 collective-permute-done.13
  148.3 6.3 %collective-permute-start.14 = (f32[3,8,18]{2,1,0:T(8,128)S(1)}, f32[3,8,18]{2,1,0:T(8,128)S(1)}, u32[]{:S(2)}, u32[]{:S(2)}) collective-permute-start(f32[3,8,18]{2,1,0:T(8,128)S(1)} %pad_maximum_fusion.17), channel_id=1, source_target_pairs={{0,1},{1,0},{2,3},{3,2},{4,5},{5,4},{6,7},{7,6},{8,9},{9,8},{10,11... | collective-permute-start | bytes 5192 | tf_op jit(solution)/shard_map/ppermute | solution.py:20
  155.6 0.9 fusion.20
  156.5 0.9 fusion.7
  158.2 1.1 fusion
  159.3 1.1 fusion.61
  160.6 2.3 collective-permute-start.15
  164.0 1.9 collective-permute-start.16
  165.9 4.1 %collective-permute-done.16 = f32[3,8,153]{2,1,0:T(8,128)S(1)} collective-permute-done((f32[3,8,153]{2,1,0:T(8,128)S(1)}, f32[3,8,153]{2,1,0:T(8,128)S(1)}, u32[]{:S(2)}, u32[]{:S(2)}) %collective-permute-start.16) | collective-permute-done | bytes 14720 | tf_op jit(solution)/shard_map/ppermute | solution.py:20
  170.2 1.9 collective-permute-start.17
  172.4 3.7 %collective-permute-done.17 = f32[3,8,34]{2,1,0:T(8,128)S(1)} collective-permute-done((f32[3,8,34]{2,1,0:T(8,128)S(1)}, f32[3,8,34]{2,1,0:T(8,128)S(1)}, u32[]{:S(2)}, u32[]{:S(2)}) %collective-permute-start.17) | collective-permute-done | bytes 3296 | tf_op jit(solution)/shard_map/ppermute | solution.py:20
  176.6 7.2 %scatter_fusion.2 = f32[3,8,128]{1,0,2:T(4,128)S(1)} fusion(f32[3,8,128]{1,0,2:T(4,128)S(1)} %copy.122, s32[178]{0:T(256)S(1)} %compare_select_fusion, f32[178,3,8]{2,1,0:T(4,128)S(1)} %copy.112), kind=kCustom, calls=%fused_computation.6 | custom fusion | flops 4272 | bytes 51976 | tf_op jit(solution)/shard_map/scatter-add | solution.py:149
  186.2 3.4 %collective-permute-start.18 = (f32[3,8,34]{2,1,0:T(8,128)S(1)}, f32[3,8,34]{2,1,0:T(8,128)S(1)}, u32[]{:S(2)}, u32[]{:S(2)}) collective-permute-start(f32[3,8,34]{2,1,0:T(8,128)S(1)} %pad_maximum_fusion.20), channel_id=1, source_target_pairs={{0,14},{2,0},{4,2},{6,4},{8,6},{10,8},{12,10},{14,12},{1,15},{3,1}... | collective-permute-start | bytes 9800 | tf_op jit(solution)/shard_map/ppermute | solution.py:20
  189.7 1.0 collective-permute-done.18
  190.9 3.4 %collective-permute-start.19 = (f32[3,8,153]{2,1,0:T(8,128)S(1)}, f32[3,8,153]{2,1,0:T(8,128)S(1)}, u32[]{:S(2)}, u32[]{:S(2)}) collective-permute-start(f32[3,8,153]{2,1,0:T(8,128)S(1)} %pad_maximum_fusion.6), channel_id=1, source_target_pairs={{0,240},{16,0},{32,16},{48,32},{64,48},{80,64},{96,80},{112,96},{1... | collective-permute-start | bytes 44072 | tf_op jit(solution)/shard_map/ppermute | solution.py:20
  194.3 1.2 collective-permute-done.19
  195.7 6.5 %collective-permute-start.20 = (f32[3,8,18]{2,1,0:T(8,128)S(1)}, f32[3,8,18]{2,1,0:T(8,128)S(1)}, u32[]{:S(2)}, u32[]{:S(2)}) collective-permute-start(f32[3,8,18]{2,1,0:T(8,128)S(1)} %pad_maximum_fusion.21), channel_id=1, source_target_pairs={{0,1},{1,0},{2,3},{3,2},{4,5},{5,4},{6,7},{7,6},{8,9},{9,8},{10,11... | collective-permute-start | bytes 5192 | tf_op jit(solution)/shard_map/ppermute | solution.py:20
  203.0 0.9 fusion.18
  203.8 0.9 fusion.5
  204.9 1.1 fusion.66
  206.4 1.1 fusion.2
  207.5 1.1 fusion.57
  208.9 2.3 collective-permute-start.21
  212.2 1.9 collective-permute-start.22
  216.6 1.6 collective-permute-done.22
  218.4 1.9 collective-permute-start.23
  221.4 3.0 %collective-permute-done.23 = f32[3,8,34]{2,1,0:T(8,128)S(1)} collective-permute-done((f32[3,8,34]{2,1,0:T(8,128)S(1)}, f32[3,8,34]{2,1,0:T(8,128)S(1)}, u32[]{:S(2)}, u32[]{:S(2)}) %collective-permute-start.23) | collective-permute-done | bytes 3296 | tf_op jit(solution)/shard_map/ppermute | solution.py:20
  224.9 7.2 %scatter_fusion.3 = f32[3,8,128]{1,0,2:T(4,128)S(1)} fusion(f32[3,8,128]{1,0,2:T(4,128)S(1)} %copy.123, s32[178]{0:T(256)S(1)} %compare_select_fusion, f32[178,3,8]{2,1,0:T(4,128)S(1)} %copy.117), kind=kCustom, calls=%fused_computation.7 | custom fusion | flops 4272 | bytes 51976 | tf_op jit(solution)/shard_map/scatter-add | solution.py:149
  232.1 1.2 multiply_reduce_fusion
  234.2 20.7 %all-gather.3 = f32[16,3,2]{1,2,0:T(2,128)S(1)} all-gather(f32[1,3,2]{1,2,0:T(2,128)S(1)} %bitcast.84), channel_id=2, replica_groups=mesh['runs'=2,'gx'=16,'gy'=8,'gz'=2] {'gx'}, dimensions={0}, use_global_device_ids=true | all-gather | bytes 408 | tf_op jit(solution)/shard_map/all_gather | solution.py:25
  255.0 11.0 %all-gather.4 = f32[8,3,2]{1,2,0:T(2,128)S(1)} all-gather(f32[1,3,2]{1,2,0:T(2,128)S(1)} %bitcast.85), channel_id=3, replica_groups=mesh['runs'=2,'gx'=16,'gy'=8,'gz'=2] {'gy'}, dimensions={0}, use_global_device_ids=true | all-gather | bytes 216 | tf_op jit(solution)/shard_map/all_gather | solution.py:25
  266.0 15.1 %all-gather.5 = f32[2,3,2]{1,2,0:T(2,128)S(1)} all-gather(f32[1,3,2]{1,2,0:T(2,128)S(1)} %bitcast.86), channel_id=4, replica_groups=mesh['runs'=2,'gx'=16,'gy'=8,'gz'=2] {'gz'}, dimensions={0}, use_global_device_ids=true | all-gather | bytes 72 | tf_op jit(solution)/shard_map/all_gather | solution.py:25
  (267 shorter events, 28.0 us)
Async XLA Ops:
  2.0 8.5 %copy-start.4 = (s32[2,1792]{1,0:T(2,128)S(1)}, s32[2,1792]{1,0:T(2,128)}, u32[]{:S(2)}) copy-start(s32[2,1792]{1,0:T(2,128)} %param.14) | copy-start | bytes 43012
  3.9 57.6 %copy-start.3 = (f32[3,178]{1,0:T(4,128)S(1)}, f32[3,178]{1,0:T(4,128)}, u32[]{:S(2)}) copy-start(f32[3,178]{1,0:T(4,128)} %constant.57.clone) | copy-start | bytes 6412
  3.9 57.7 %copy-start = (f32[3,8,128]{2,1,0:T(8,128)S(1)}, f32[3,8,128]{2,1,0:T(8,128)}, u32[]{:S(2)}) copy-start(f32[3,8,128]{2,1,0:T(8,128)} %param.11) | copy-start | bytes 36868
  4.1 7.1 %collective-permute-start = (f32[3,8,34]{2,1,0:T(8,128)S(1)}, f32[3,8,34]{2,1,0:T(8,128)S(1)}, u32[]{:S(2)}, u32[]{:S(2)}) collective-permute-start(f32[3,8,34]{2,1,0:T(8,128)S(1)} %pad_maximum_fusion.8), channel_id=1, source_target_pairs={{0,14},{2,0},{4,2},{6,4},{8,6},{10,8},{12,10},{14,12},{1,15},{3,1}... | collective-permute-start | bytes 9800 | tf_op jit(solution)/shard_map/ppermute | solution.py:20
  11.5 44.7 %collective-permute-start.1 = (f32[3,8,153]{2,1,0:T(8,128)S(1)}, f32[3,8,153]{2,1,0:T(8,128)S(1)}, u32[]{:S(2)}, u32[]{:S(2)}) collective-permute-start(f32[3,8,153]{2,1,0:T(8,128)S(1)} %pad_maximum_fusion), channel_id=1, source_target_pairs={{0,240},{16,0},{32,16},{48,32},{64,48},{80,64},{96,80},{112,96},{1... | collective-permute-start | bytes 44072 | tf_op jit(solution)/shard_map/ppermute | solution.py:20
  56.3 5.1 %collective-permute-start.2 = (f32[3,8,18]{2,1,0:T(8,128)S(1)}, f32[3,8,18]{2,1,0:T(8,128)S(1)}, u32[]{:S(2)}, u32[]{:S(2)}) collective-permute-start(f32[3,8,18]{2,1,0:T(8,128)S(1)} %pad_maximum_fusion.9), channel_id=1, source_target_pairs={{0,1},{1,0},{2,3},{3,2},{4,5},{5,4},{6,7},{7,6},{8,9},{9,8},{10,11... | collective-permute-start | bytes 5192 | tf_op jit(solution)/shard_map/ppermute | solution.py:20
  65.2 13.2 %copy-start.1 = (s32[7,128]{1,0:T(8,128)S(1)}, s32[7,128]{1,0:T(8,128)}, u32[]{:S(2)}) copy-start(s32[7,128]{1,0:T(8,128)} %param.15) | copy-start | bytes 10756
  66.6 3.1 %collective-permute-start.3 = (f32[3,8,18]{2,1,0:T(8,128)S(1)}, f32[3,8,18]{2,1,0:T(8,128)S(1)}, u32[]{:S(2)}, u32[]{:S(2)}) collective-permute-start(f32[3,8,18]{2,1,0:T(8,128)S(1)} %pad_maximum_fusion.10), channel_id=1, source_target_pairs={{0,1},{1,0},{2,3},{3,2},{4,5},{5,4},{6,7},{7,6},{8,9},{9,8},{10,11... | collective-permute-start | bytes 5192 | tf_op jit(solution)/shard_map/ppermute | solution.py:20
  69.9 6.4 %collective-permute-start.4 = (f32[3,8,153]{2,1,0:T(8,128)S(1)}, f32[3,8,153]{2,1,0:T(8,128)S(1)}, u32[]{:S(2)}, u32[]{:S(2)}) collective-permute-start(f32[3,8,153]{2,1,0:T(8,128)S(1)} %pad_maximum_fusion.1), channel_id=1, source_target_pairs={{0,16},{16,32},{32,48},{48,64},{64,80},{80,96},{96,112},{112,128},... | collective-permute-start | bytes 44072 | tf_op jit(solution)/shard_map/ppermute | solution.py:20
  76.5 6.2 %collective-permute-start.5 = (f32[3,8,34]{2,1,0:T(8,128)S(1)}, f32[3,8,34]{2,1,0:T(8,128)S(1)}, u32[]{:S(2)}, u32[]{:S(2)}) collective-permute-start(f32[3,8,34]{2,1,0:T(8,128)S(1)} %pad_maximum_fusion.11), channel_id=1, source_target_pairs={{0,2},{2,4},{4,6},{6,8},{8,10},{10,12},{12,14},{14,0},{1,3},{3,5},... | collective-permute-start | bytes 9800 | tf_op jit(solution)/shard_map/ppermute | solution.py:20
  78.7 11.7 %copy-start.5 = (f32[3,8,128]{2,1,0:T(8,128)S(1)}, f32[3,8,128]{2,1,0:T(8,128)}, u32[]{:S(2)}) copy-start(f32[3,8,128]{2,1,0:T(8,128)} %param.12) | copy-start | bytes 36868
  92.1 4.5 %collective-permute-start.6 = (f32[3,8,34]{2,1,0:T(8,128)S(1)}, f32[3,8,34]{2,1,0:T(8,128)S(1)}, u32[]{:S(2)}, u32[]{:S(2)}) collective-permute-start(f32[3,8,34]{2,1,0:T(8,128)S(1)} %pad_maximum_fusion.12), channel_id=1, source_target_pairs={{0,14},{2,0},{4,2},{6,4},{8,6},{10,8},{12,10},{14,12},{1,15},{3,1}... | collective-permute-start | bytes 9800 | tf_op jit(solution)/shard_map/ppermute | solution.py:20
  96.8 4.6 %collective-permute-start.7 = (f32[3,8,153]{2,1,0:T(8,128)S(1)}, f32[3,8,153]{2,1,0:T(8,128)S(1)}, u32[]{:S(2)}, u32[]{:S(2)}) collective-permute-start(f32[3,8,153]{2,1,0:T(8,128)S(1)} %pad_maximum_fusion.2), channel_id=1, source_target_pairs={{0,240},{16,0},{32,16},{48,32},{64,48},{80,64},{96,80},{112,96},{1... | collective-permute-start | bytes 44072 | tf_op jit(solution)/shard_map/ppermute | solution.py:20
  101.6 7.1 %collective-permute-start.8 = (f32[3,8,18]{2,1,0:T(8,128)S(1)}, f32[3,8,18]{2,1,0:T(8,128)S(1)}, u32[]{:S(2)}, u32[]{:S(2)}) collective-permute-start(f32[3,8,18]{2,1,0:T(8,128)S(1)} %pad_maximum_fusion.13), channel_id=1, source_target_pairs={{0,1},{1,0},{2,3},{3,2},{4,5},{5,4},{6,7},{7,6},{8,9},{9,8},{10,11... | collective-permute-start | bytes 5192 | tf_op jit(solution)/shard_map/ppermute | solution.py:20
  113.9 3.1 %collective-permute-start.9 = (f32[3,8,18]{2,1,0:T(8,128)S(1)}, f32[3,8,18]{2,1,0:T(8,128)S(1)}, u32[]{:S(2)}, u32[]{:S(2)}) collective-permute-start(f32[3,8,18]{2,1,0:T(8,128)S(1)} %pad_maximum_fusion.14), channel_id=1, source_target_pairs={{0,1},{1,0},{2,3},{3,2},{4,5},{5,4},{6,7},{7,6},{8,9},{9,8},{10,11... | collective-permute-start | bytes 5192 | tf_op jit(solution)/shard_map/ppermute | solution.py:20
  117.2 6.1 %collective-permute-start.10 = (f32[3,8,153]{2,1,0:T(8,128)S(1)}, f32[3,8,153]{2,1,0:T(8,128)S(1)}, u32[]{:S(2)}, u32[]{:S(2)}) collective-permute-start(f32[3,8,153]{2,1,0:T(8,128)S(1)} %pad_maximum_fusion.3), channel_id=1, source_target_pairs={{0,16},{16,32},{32,48},{48,64},{64,80},{80,96},{96,112},{112,128},... | collective-permute-start | bytes 44072 | tf_op jit(solution)/shard_map/ppermute | solution.py:20
  123.5 6.0 %collective-permute-start.11 = (f32[3,8,34]{2,1,0:T(8,128)S(1)}, f32[3,8,34]{2,1,0:T(8,128)S(1)}, u32[]{:S(2)}, u32[]{:S(2)}) collective-permute-start(f32[3,8,34]{2,1,0:T(8,128)S(1)} %pad_maximum_fusion.15), channel_id=1, source_target_pairs={{0,2},{2,4},{4,6},{6,8},{8,10},{10,12},{12,14},{14,0},{1,3},{3,5},... | collective-permute-start | bytes 9800 | tf_op jit(solution)/shard_map/ppermute | solution.py:20
  138.9 4.5 %collective-permute-start.12 = (f32[3,8,34]{2,1,0:T(8,128)S(1)}, f32[3,8,34]{2,1,0:T(8,128)S(1)}, u32[]{:S(2)}, u32[]{:S(2)}) collective-permute-start(f32[3,8,34]{2,1,0:T(8,128)S(1)} %pad_maximum_fusion.16), channel_id=1, source_target_pairs={{0,14},{2,0},{4,2},{6,4},{8,6},{10,8},{12,10},{14,12},{1,15},{3,1}... | collective-permute-start | bytes 9800 | tf_op jit(solution)/shard_map/ppermute | solution.py:20
  143.6 4.6 %collective-permute-start.13 = (f32[3,8,153]{2,1,0:T(8,128)S(1)}, f32[3,8,153]{2,1,0:T(8,128)S(1)}, u32[]{:S(2)}, u32[]{:S(2)}) collective-permute-start(f32[3,8,153]{2,1,0:T(8,128)S(1)} %pad_maximum_fusion.4), channel_id=1, source_target_pairs={{0,240},{16,0},{32,16},{48,32},{64,48},{80,64},{96,80},{112,96},{1... | collective-permute-start | bytes 44072 | tf_op jit(solution)/shard_map/ppermute | solution.py:20
  148.3 7.1 %collective-permute-start.14 = (f32[3,8,18]{2,1,0:T(8,128)S(1)}, f32[3,8,18]{2,1,0:T(8,128)S(1)}, u32[]{:S(2)}, u32[]{:S(2)}) collective-permute-start(f32[3,8,18]{2,1,0:T(8,128)S(1)} %pad_maximum_fusion.17), channel_id=1, source_target_pairs={{0,1},{1,0},{2,3},{3,2},{4,5},{5,4},{6,7},{7,6},{8,9},{9,8},{10,11... | collective-permute-start | bytes 5192 | tf_op jit(solution)/shard_map/ppermute | solution.py:20
  160.6 3.1 %collective-permute-start.15 = (f32[3,8,18]{2,1,0:T(8,128)S(1)}, f32[3,8,18]{2,1,0:T(8,128)S(1)}, u32[]{:S(2)}, u32[]{:S(2)}) collective-permute-start(f32[3,8,18]{2,1,0:T(8,128)S(1)} %pad_maximum_fusion.18), channel_id=1, source_target_pairs={{0,1},{1,0},{2,3},{3,2},{4,5},{5,4},{6,7},{7,6},{8,9},{9,8},{10,11... | collective-permute-start | bytes 5192 | tf_op jit(solution)/shard_map/ppermute | solution.py:20
  164.0 6.1 %collective-permute-start.16 = (f32[3,8,153]{2,1,0:T(8,128)S(1)}, f32[3,8,153]{2,1,0:T(8,128)S(1)}, u32[]{:S(2)}, u32[]{:S(2)}) collective-permute-start(f32[3,8,153]{2,1,0:T(8,128)S(1)} %pad_maximum_fusion.5), channel_id=1, source_target_pairs={{0,16},{16,32},{32,48},{48,64},{64,80},{80,96},{96,112},{112,128},... | collective-permute-start | bytes 44072 | tf_op jit(solution)/shard_map/ppermute | solution.py:20
  170.2 6.0 %collective-permute-start.17 = (f32[3,8,34]{2,1,0:T(8,128)S(1)}, f32[3,8,34]{2,1,0:T(8,128)S(1)}, u32[]{:S(2)}, u32[]{:S(2)}) collective-permute-start(f32[3,8,34]{2,1,0:T(8,128)S(1)} %pad_maximum_fusion.19), channel_id=1, source_target_pairs={{0,2},{2,4},{4,6},{6,8},{8,10},{10,12},{12,14},{14,0},{1,3},{3,5},... | collective-permute-start | bytes 9800 | tf_op jit(solution)/shard_map/ppermute | solution.py:20
  184.8 47.3 %copy-start.2 = (f32[3,8,128]{2,1,0:T(8,128)}, f32[3,8,128]{2,1,0:T(8,128)S(1)}, u32[]{:S(2)}) copy-start(f32[3,8,128]{2,1,0:T(8,128)S(1)} %pad_add_fusion) | copy-start | bytes 36868
  186.2 4.5 %collective-permute-start.18 = (f32[3,8,34]{2,1,0:T(8,128)S(1)}, f32[3,8,34]{2,1,0:T(8,128)S(1)}, u32[]{:S(2)}, u32[]{:S(2)}) collective-permute-start(f32[3,8,34]{2,1,0:T(8,128)S(1)} %pad_maximum_fusion.20), channel_id=1, source_target_pairs={{0,14},{2,0},{4,2},{6,4},{8,6},{10,8},{12,10},{14,12},{1,15},{3,1}... | collective-permute-start | bytes 9800 | tf_op jit(solution)/shard_map/ppermute | solution.py:20
  190.9 4.6 %collective-permute-start.19 = (f32[3,8,153]{2,1,0:T(8,128)S(1)}, f32[3,8,153]{2,1,0:T(8,128)S(1)}, u32[]{:S(2)}, u32[]{:S(2)}) collective-permute-start(f32[3,8,153]{2,1,0:T(8,128)S(1)} %pad_maximum_fusion.6), channel_id=1, source_target_pairs={{0,240},{16,0},{32,16},{48,32},{64,48},{80,64},{96,80},{112,96},{1... | collective-permute-start | bytes 44072 | tf_op jit(solution)/shard_map/ppermute | solution.py:20
  195.7 7.1 %collective-permute-start.20 = (f32[3,8,18]{2,1,0:T(8,128)S(1)}, f32[3,8,18]{2,1,0:T(8,128)S(1)}, u32[]{:S(2)}, u32[]{:S(2)}) collective-permute-start(f32[3,8,18]{2,1,0:T(8,128)S(1)} %pad_maximum_fusion.21), channel_id=1, source_target_pairs={{0,1},{1,0},{2,3},{3,2},{4,5},{5,4},{6,7},{7,6},{8,9},{9,8},{10,11... | collective-permute-start | bytes 5192 | tf_op jit(solution)/shard_map/ppermute | solution.py:20
  208.9 3.1 %collective-permute-start.21 = (f32[3,8,18]{2,1,0:T(8,128)S(1)}, f32[3,8,18]{2,1,0:T(8,128)S(1)}, u32[]{:S(2)}, u32[]{:S(2)}) collective-permute-start(f32[3,8,18]{2,1,0:T(8,128)S(1)} %pad_maximum_fusion.22), channel_id=1, source_target_pairs={{0,1},{1,0},{2,3},{3,2},{4,5},{5,4},{6,7},{7,6},{8,9},{9,8},{10,11... | collective-permute-start | bytes 5192 | tf_op jit(solution)/shard_map/ppermute | solution.py:20
  212.2 6.1 %collective-permute-start.22 = (f32[3,8,153]{2,1,0:T(8,128)S(1)}, f32[3,8,153]{2,1,0:T(8,128)S(1)}, u32[]{:S(2)}, u32[]{:S(2)}) collective-permute-start(f32[3,8,153]{2,1,0:T(8,128)S(1)} %pad_maximum_fusion.7), channel_id=1, source_target_pairs={{0,16},{16,32},{32,48},{48,64},{64,80},{80,96},{96,112},{112,128},... | collective-permute-start | bytes 44072 | tf_op jit(solution)/shard_map/ppermute | solution.py:20
  218.4 6.0 %collective-permute-start.23 = (f32[3,8,34]{2,1,0:T(8,128)S(1)}, f32[3,8,34]{2,1,0:T(8,128)S(1)}, u32[]{:S(2)}, u32[]{:S(2)}) collective-permute-start(f32[3,8,34]{2,1,0:T(8,128)S(1)} %pad_maximum_fusion.23), channel_id=1, source_target_pairs={{0,2},{2,4},{4,6},{6,8},{8,10},{10,12},{12,14},{14,0},{1,3},{3,5},... | collective-permute-start | bytes 9800 | tf_op jit(solution)/shard_map/ppermute | solution.py:20
